TPU v7x, 512 devices: a whole 4x4x16 slice. The times are simulated.
512 devices in a mesh: dp: 64 (over y, z), mp: 8 (over x, core).
Axes of the slice: x: 4, y: 4, z: 16, core: 2. Of those that a mesh axis runs over, the one named last changes fastest.
Arguments:
- tokens: bfloat16 [512, 8192], P('mp', 'dp'), may hold values from -6 to 6
- norm_gain: float32 [8192], replicated, may hold values from 0.25 to 1.75
- query_weight: bfloat16 [8192, 8192], P(None, 'dp'), may hold values from -0.0625 to 0.0625
- out_weight: bfloat16 [8192, 8192], P(None, 'dp'), may hold values from -0.0625 to 0.0625
- gate_scalar: float32 [1], replicated, may hold values from 0.4 to 1.5
- image_keys: bfloat16 [128, 64, 8192], P('mp', None, 'dp'), may hold values from -260 to 260
- image_values: bfloat16 [128, 64, 8192], P('mp', None, 'dp'), may hold values from -6 to 6
- active_image: int32 [128, 4], replicated, may hold values from 0 to 127
- image_slot: int32 [128], replicated, may hold values from 0 to 127, each once
Outputs:
- mixed: bfloat16 [512, 8192], P('mp', 'dp')
Inputs may be any that keep to these rules, and one draw needn't show every extreme that they name: `image_slot`: each slot 0 to 127 once.
All inputs are finite; a program needn't handle non-finite values.
Results may differ from a plain program's by a relative error of at most 0.0047.
Values may be sent and summed in bfloat16 or wider, within the bound.
A program may use at most 64 MiB of HBM per device.

v0:
```python
import jax
import jax.numpy as jnp
from jax import lax
from jax.sharding import Mesh
from jax.sharding import PartitionSpec as P

DP = ("dp_0", "dp_1")
epsilon = 1e-05


def laid_out(parts, dim):
    lengths = list(parts.shape[1:])
    lengths[dim] *= parts.shape[0]
    return jnp.moveaxis(parts, 0, dim).reshape(lengths)


def gather_in_order(value, axes, sequence):
    parts = value[None]
    for k in sequence:
        parts = lax.all_gather(parts, axes[k], axis=0, tiled=True)
    carried = [lax.axis_size(axes[k]) for k in reversed(sequence)]
    parts = parts.reshape(*carried, *value.shape)
    turned = sorted(range(len(sequence)), key=lambda place: sequence[len(sequence) - 1 - place])
    return parts.transpose(*turned, *range(len(sequence), parts.ndim)).reshape(-1, *value.shape)


def whole_of(value, axes, sequence, dim):
    return laid_out(gather_in_order(value, axes, sequence), dim)


def from_everyone(value, axis):
    copies = jnp.broadcast_to(value, (lax.axis_size(axis), *value.shape))
    return lax.all_to_all(copies, axis, split_axis=0, concat_axis=0, tiled=True)


def gathered_copies(value, axis, dim):
    parts = from_everyone(value, axis)
    return laid_out(parts, dim)


def split_up(value, dim, peers):
    lengths = value.shape
    parts = value.reshape(*lengths[:dim], peers, lengths[dim] // peers, *lengths[dim + 1 :])
    return jnp.moveaxis(parts, dim, 0)


def sent_and_summed(value, axis, dim):
    peers = lax.axis_size(axis)
    parts = lax.all_to_all(split_up(value, dim, peers), axis, 0, 0, tiled=True)
    return jnp.sum(parts.astype(jnp.float32), axis=0)


def attend(queries, wanted, keys_block, values_block, first_slot):
    visual = keys_block.shape[1]
    width = keys_block.shape[2]
    flat_keys = keys_block.reshape(-1, width)
    flat_values = values_block.reshape(-1, width)
    scores = lax.dot_general(
        queries, flat_keys, (((1,), (1,)), ((), ())), preferred_element_type=jnp.float32
    ) * width ** (-0.5)
    column_slot = first_slot + jnp.arange(flat_keys.shape[0], dtype=jnp.int32) // visual
    matches = wanted[:, None] == column_slot[None, :]
    owned = jnp.any(matches, axis=1, keepdims=True)
    masked = jnp.where(matches, scores, -1e30)
    largest = jnp.max(masked, axis=1, keepdims=True)
    expo = jnp.where(matches, jnp.exp(masked - largest), 0.0)
    totals = jnp.where(owned, jnp.sum(expo, axis=1, keepdims=True), 1.0)
    rounded = (expo / totals).astype(jnp.bfloat16)
    result = jnp.dot(rounded, flat_values, preferred_element_type=jnp.float32)
    return jnp.where(owned, result, 0.0)


def body(
    tokens,
    norm_gain,
    query_weight,
    out_weight,
    gate_scalar,
    image_keys,
    image_values,
    active_image,
    image_slot,
):
    whole = whole_of(tokens, DP, (0, 1), 1)
    widened = whole.astype(jnp.float32)
    average = jnp.mean(widened, axis=1, keepdims=True)
    centred = widened - average
    variance = jnp.mean(centred * centred, axis=1, keepdims=True)
    normed = (centred * lax.rsqrt(variance + epsilon) * norm_gain).astype(jnp.bfloat16)
    queries = jnp.dot(normed, query_weight, preferred_element_type=jnp.float32).astype(jnp.bfloat16)
    slots_all = image_slot[active_image.reshape(-1)]
    owned_slots = image_keys.shape[0]
    every_query = gathered_copies(queries, "mp", 0)
    first_slot = lax.axis_index("mp") * owned_slots
    gathered = sent_and_summed(
        attend(every_query, slots_all, image_keys, image_values, first_slot).astype(jnp.bfloat16),
        "mp",
        0,
    )
    attended = gathered.astype(jnp.bfloat16)
    projected = jnp.dot(
        whole_of(attended, DP, (0, 1), 1), out_weight, preferred_element_type=jnp.float32
    )
    result = tokens.astype(jnp.float32) + jnp.tanh(gate_scalar[0]) * projected
    return result.astype(jnp.bfloat16)


def solution(mesh):
    split = Mesh(mesh.devices.reshape(4, 16, mesh.shape["mp"]), ("dp_0", "dp_1", "mp"))
    placed = (
        P("mp", DP),
        P(),
        P(None, DP),
        P(None, DP),
        P(),
        P("mp", None, DP),
        P("mp", None, DP),
        P(),
        P(),
    )
    return jax.shard_map(body, mesh=split, in_specs=placed, out_specs=P("mp", DP), check_vma=False)
```

profile of v0, /device:TPU:2, one launch (start us, length us, event | category | flops | bytes accessed | tf_op | source)
XLA Modules:
  0.0 209.5 jit_solution(14668221166612236900)
XLA Ops:
  6.5 0.0 copy-start
  6.5 0.0 all-gather.5.cloned.1.call-start
  6.5 14.0 %all-gather = bf16[256,128]{1,0:T(8,128)(2,1)} all-gather(bf16[64,128]{1,0:T(8,128)(2,1)} %param.9), channel_id=2, replica_groups=mesh['dp_0'=4,'dp_1'=16,'mp'=8] {'dp_0'}, dimensions={0}, use_global_device_ids=true | all-gather | bytes 81920 | tf_op jit(solution)/shard_map/all_gather | solution.py:20
  20.6 0.0 all-gather.5.cloned.1.call-update
  20.6 0.8 copy.18
  21.4 0.1 reshape.104
  21.5 3.4 %gather_fusion = s32[512]{0:T(512)S(1)} fusion(s32[128]{0:T(128)} %param.17, s32[1024]{0:T(1024)S(1)} %pad_clamp_fusion), kind=kCustom, calls=%fused_computation | custom fusion | bytes 6144 | tf_op jit(solution)/shard_map/gather | solution.py:91
  25.0 69.7 %all-gather.5.cloned.1.call-done = bf16[64,64,128]{2,1,0:T(8,128)(2,1)} async-done(((bf16[4,64,128]{2,1,0:T(8,128)(2,1)}), bf16[64,64,128]{2,1,0:T(8,128)(2,1)}) %all-gather.5.cloned.1.call-update) | async-done | bytes 1048592 | tf_op jit(solution)/shard_map/all_gather | solution.py:20
  94.6 1.5 convert_reduce_fusion
  96.1 1.5 convert_element_type.65
  97.6 0.2 copy.19
  97.9 0.0 copy-start.3
  97.9 0.4 fusion.4
  98.3 0.0 copy-done
  98.3 0.3 copy-done.3
  98.6 0.0 copy-start.4
  98.6 0.6 convolution_convert_fusion
  99.2 0.7 broadcast_in_dim.43
  99.9 4.8 %all-to-all-start = ((bf16[8,64,128]{2,1,0:T(8,128)(2,1)}), bf16[8,64,128]{2,1,0:T(8,128)(2,1)S(1)}, u32[]{:S(2)}, u32[]{:S(2)}) async-start(bf16[8,64,128]{2,1,0:T(8,128)(2,1)} %broadcast_in_dim.43), calls=%async_computation | async-start | bytes 262144 | tf_op jit(solution)/shard_map/all_to_all | solution.py:33
  104.7 0.0 all-gather.7.cloned.1.call-start
  104.7 0.4 compare_reduce_fusion
  105.1 4.3 %all-to-all-done = bf16[8,64,128]{2,1,0:T(8,128)(2,1)S(1)} async-done(((bf16[8,64,128]{2,1,0:T(8,128)(2,1)}), bf16[8,64,128]{2,1,0:T(8,128)(2,1)S(1)}, u32[]{:S(2)}, u32[]{:S(2)}) %all-to-all-start) | async-done | bytes 131104 | tf_op jit(solution)/shard_map/all_to_all | solution.py:33
  109.3 0.0 copy-done.4
  109.3 0.0 copy-start.5
  109.3 0.5 fusion.5
  109.9 0.7 fusion.6
  110.6 0.0 copy-done.5
  110.6 1.2 fusion.7
  111.8 0.0 copy-start.2
  111.8 8.5 %all_to_all.10 = bf16[8,64,128]{2,1,0:T(8,128)(2,1)S(1)} all-to-all(bf16[8,64,128]{2,1,0:T(8,128)(2,1)S(1)} %bitcast.51), channel_id=1, replica_groups=mesh['dp_0'=4,'dp_1'=16,'mp'=8] {'mp'}, dimensions={0} | all-to-all | bytes 262144 | tf_op jit(solution)/shard_map/all_to_all | solution.py:49
  120.4 12.9 %all-gather.1 = bf16[256,128]{1,0:T(8,128)(2,1)} all-gather(bf16[64,128]{1,0:T(8,128)(2,1)S(1)} %reduce_sum.42), channel_id=3, replica_groups=mesh['dp_0'=4,'dp_1'=16,'mp'=8] {'dp_0'}, dimensions={0}, use_global_device_ids=true | all-gather | bytes 81920 | tf_op jit(solution)/shard_map/all_gather | solution.py:20
  133.3 0.0 all-gather.7.cloned.1.call-update
  134.0 65.6 %all-gather.7.cloned.1.call-done = bf16[64,64,128]{2,1,0:T(8,128)(2,1)} async-done(((bf16[4,64,128]{2,1,0:T(8,128)(2,1)}), bf16[64,64,128]{2,1,0:T(8,128)(2,1)}) %all-gather.7.cloned.1.call-update) | async-done | bytes 1048592 | tf_op jit(solution)/shard_map/all_gather | solution.py:20
  199.6 0.0 copy-start.1
  199.6 1.5 copy.21
  201.1 0.0 copy-done.2
  201.1 0.4 copy-done.1
  201.5 1.1 fusion.9
  (7 shorter events, 0.1 us)
Async XLA Ops:
  6.5 91.8 %copy-start = (bf16[8192,128]{1,0:T(8,128)(2,1)S(1)}, bf16[8192,128]{1,0:T(8,128)(2,1)}, u32[]{:S(2)}) copy-start(bf16[8192,128]{1,0:T(8,128)(2,1)} %param.11) | copy-start | bytes 6291460
  6.5 88.1 %all-gather.5.cloned.1.call-start = ((), (), s32[]{:S(2)}) async-start(), calls=%async_computation.2 | async-start | bytes 1114112 | tf_op jit(solution)/shard_map/all_gather | solution.py:20
  97.9 0.8 copy-start.3
  98.6 10.7 %copy-start.4 = (bf16[16,64,128]{2,1,0:T(8,128)(2,1)S(1)}, bf16[16,64,128]{2,1,0:T(8,128)(2,1)}, u32[]{:S(2)}) copy-start(bf16[16,64,128]{2,1,0:T(8,128)(2,1)} %param.14) | copy-start | bytes 786436
  99.9 9.4 %all-to-all-start = ((bf16[8,64,128]{2,1,0:T(8,128)(2,1)}), bf16[8,64,128]{2,1,0:T(8,128)(2,1)S(1)}, u32[]{:S(2)}, u32[]{:S(2)}) async-start(bf16[8,64,128]{2,1,0:T(8,128)(2,1)} %broadcast_in_dim.43), calls=%async_computation | async-start | bytes 262144 | tf_op jit(solution)/shard_map/all_to_all | solution.py:33
  104.7 95.0 %all-gather.7.cloned.1.call-start = ((), (), s32[]{:S(2)}) async-start(), calls=%async_computation.3 | async-start | bytes 1114112 | tf_op jit(solution)/shard_map/all_gather | solution.py:20
  109.3 1.3 copy-start.5
  111.8 89.3 %copy-start.2 = (bf16[64,128]{1,0:T(8,128)(2,1)S(1)}, bf16[64,128]{1,0:T(8,128)(2,1)}, u32[]{:S(2)}) copy-start(bf16[64,128]{1,0:T(8,128)(2,1)} %param.9) | copy-start | bytes 49156
  199.6 1.9 copy-start.1
Sparse Core Ops, SparseCore 0:
  20.7 73.8 all-gather.4
  133.4 66.1 all-gather.6
where the time goes:
time: 210 us
  waiting for transfers between devices  140 us (67%)
  blocking collectives  35.5 us (17%)
  between operations  14.2 us (7%)
  local copies, waits for them, and re-layouts  7.49 us (4%)
  starting transfers between devices  4.81 us (2%)
  other arithmetic  4.52 us (2%)
  matrix products  3.47 us (2%)
    all_gather x2, waiting for transfers between devices, gather_in_order(): parts = lax.all_gather(parts, axes[k], axis=0, tiled=True)  135 us
    all_gather x2, blocking collectives, gather_in_order(): parts = lax.all_gather(parts, axes[k], axis=0, tiled=True)  27 us
    all_to_all x1, blocking collectives, sent_and_summed(): parts = lax.all_to_all(split_up(value, dim, peers), axis, 0, 0, tiled=True)  8.49 us
    all_to_all x1, starting transfers between devices, from_everyone(): return lax.all_to_all(copies, axis, split_axis=0, concat_axis=0, tiled=True)  4.8 us
    all_to_all x1, waiting for transfers between devices, from_everyone(): return lax.all_to_all(copies, axis, split_axis=0, concat_axis=0, tiled=True)  4.26 us
  transfers between devices with their start and end apart: 3, of which 3 were waited for; matrix products, arithmetic and copies ran while one was open for 2% of the time, Pallas kernels for 0%

commit v1 on v0

--- a/solution.py
+++ b/solution.py
@@ -17,7 +17,9 @@
 def gather_in_order(value, axes, sequence):
     parts = value[None]
     for k in sequence:
-        parts = lax.all_gather(parts, axes[k], axis=0, tiled=True)
+        parts = jnp.concatenate(
+            lax.all_to_all(jnp.stack([parts] * lax.axis_size(axes[k])), axes[k], 0, 0), axis=0
+        )
     carried = [lax.axis_size(axes[k]) for k in reversed(sequence)]
     parts = parts.reshape(*carried, *value.shape)
     turned = sorted(range(len(sequence)), key=lambda place: sequence[len(sequence) - 1 - place])

time: 210 us -> 168 us (0.80)
  the two profiles are of different devices: /device:TPU:2 before, /device:TPU:64 now
where the time goes in v1:
time: 168 us; the launch traced here: 167 us
  waiting for transfers between devices  97.1 us (58%)
  starting transfers between devices  27.7 us (16%)
  blocking collectives  26.5 us (16%)
  local copies, waits for them, and re-layouts  9.28 us (6%)
  matrix products  3.47 us (2%)
  other arithmetic  2.05 us (1%)
    all_to_all x2, waiting for transfers between devices, gather_in_order(): lax.all_to_all(jnp.stack([parts] * lax.axis_size(axes[k])), axes[k], 0, 0)  91.4 us
    all_to_all x2, starting transfers between devices, gather_in_order(): lax.all_to_all(jnp.stack([parts] * lax.axis_size(axes[k])), axes[k], 0, 0)  23.4 us
    all_to_all x2, blocking collectives, gather_in_order(): lax.all_to_all(jnp.stack([parts] * lax.axis_size(axes[k])), axes[k], 0, 0)  18 us
    all_to_all x1, blocking collectives, sent_and_summed(): parts = lax.all_to_all(split_up(value, dim, peers), axis, 0, 0, tiled=True)  8.49 us
    all_to_all x1, waiting for transfers between devices, from_everyone(): return lax.all_to_all(copies, axis, split_axis=0, concat_axis=0, tiled=True)  5.72 us
    all_to_all x1, starting transfers between devices, from_everyone(): return lax.all_to_all(copies, axis, split_axis=0, concat_axis=0, tiled=True)  4.3 us
    another operation x4, local copies, waits for them, and re-layouts, gather_in_order(): jnp.stack([parts] * lax.axis_size(axes[k]))  3.37 us
  transfers between devices with their start and end apart: 3, of which 3 were waited for; matrix products, arithmetic and copies ran while one was open for 2% of the time, Pallas kernels for 0%

profile of v1, /device:TPU:64, one launch (start us, length us, event | category | flops | bytes accessed | tf_op | source)
XLA Modules:
  0.0 166.9 jit_solution(5476381421377671626)
XLA Ops:
  0.0 0.0 copy-start
  0.0 0.0 copy-start.5
  0.0 0.0 copy-start.1
  0.0 0.9 stack.12
  0.9 9.9 %all_to_all.30 = bf16[4,1,64,128]{3,2,1,0:T(8,128)(2,1)S(1)} all-to-all(bf16[4,1,64,128]{3,2,1,0:T(8,128)(2,1)S(1)} %stack.12), channel_id=1, replica_groups=mesh['dp_0'=4,'dp_1'=16,'mp'=8] {'dp_0'}, dimensions={0} | all-to-all | bytes 131072 | tf_op jit(solution)/shard_map/all_to_all | solution.py:21
  10.8 1.2 stack.13
  12.0 14.8 %all-to-all-start.1 = ((bf16[16,4,64,128]{3,2,1,0:T(8,128)(2,1)}), bf16[16,4,64,128]{3,2,1,0:T(8,128)(2,1)S(1)}, u32[]{:S(2)}, u32[]{:S(2)}) async-start(bf16[16,4,64,128]{3,2,1,0:T(8,128)(2,1)} %stack.13), calls=%async_computation.1 | async-start | bytes 2097152 | tf_op jit(solution)/shard_map/all_to_all | solution.py:21
  26.8 0.0 copy-done.5
  26.8 0.1 copy.13
  26.9 0.1 reshape.106
  27.0 0.0 copy-done.1
  27.0 3.3 %gather_fusion = s32[512]{0:T(512)S(1)} fusion(s32[128]{0:T(128)S(1)} %copy-done.1, s32[1024]{0:T(1024)S(1)} %pad_clamp_fusion), kind=kCustom, calls=%fused_computation | custom fusion | bytes 6144 | tf_op jit(solution)/shard_map/gather | solution.py:93
  30.4 44.2 %all-to-all-done.1 = bf16[16,4,64,128]{3,2,1,0:T(8,128)(2,1)S(1)} async-done(((bf16[16,4,64,128]{3,2,1,0:T(8,128)(2,1)}), bf16[16,4,64,128]{3,2,1,0:T(8,128)(2,1)S(1)}, u32[]{:S(2)}, u32[]{:S(2)}) %all-to-all-start.1) | async-done | bytes 1048608 | tf_op jit(solution)/shard_map/all_to_all | solution.py:21
  74.6 0.3 fusion.16
  74.9 0.0 copy-start.4
  74.9 0.2 copy_convert_fusion
  75.1 0.4 fusion.4
  75.5 0.0 copy-done
  75.5 0.1 copy-done.4
  75.6 0.0 copy-start.6
  75.6 0.6 convolution_convert_fusion
  76.2 0.7 broadcast_in_dim.36
  76.8 4.3 %all-to-all-start.2 = ((bf16[8,64,128]{2,1,0:T(8,128)(2,1)}), bf16[8,64,128]{2,1,0:T(8,128)(2,1)S(1)}, u32[]{:S(2)}, u32[]{:S(2)}) async-start(bf16[8,64,128]{2,1,0:T(8,128)(2,1)} %broadcast_in_dim.36), calls=%async_computation.2 | async-start | bytes 262144 | tf_op jit(solution)/shard_map/all_to_all | solution.py:35
  81.1 0.4 compare_reduce_fusion
  81.5 5.7 %all-to-all-done.2 = bf16[8,64,128]{2,1,0:T(8,128)(2,1)S(1)} async-done(((bf16[8,64,128]{2,1,0:T(8,128)(2,1)}), bf16[8,64,128]{2,1,0:T(8,128)(2,1)S(1)}, u32[]{:S(2)}, u32[]{:S(2)}) %all-to-all-start.2) | async-done | bytes 131104 | tf_op jit(solution)/shard_map/all_to_all | solution.py:35
  87.2 0.0 copy-done.6
  87.2 0.0 copy-start.7
  87.2 0.5 fusion.5
  87.8 0.7 fusion.6
  88.5 0.0 copy-done.7
  88.5 1.2 fusion.7
  89.7 8.5 %all_to_all.31 = bf16[8,64,128]{2,1,0:T(8,128)(2,1)S(1)} all-to-all(bf16[8,64,128]{2,1,0:T(8,128)(2,1)S(1)} %bitcast.47), channel_id=1, replica_groups=mesh['dp_0'=4,'dp_1'=16,'mp'=8] {'mp'}, dimensions={0} | all-to-all | bytes 262144 | tf_op jit(solution)/shard_map/all_to_all | solution.py:51
  98.3 8.2 %all_to_all.32 = bf16[4,1,64,128]{3,2,1,0:T(8,128)(2,1)S(1)} all-to-all(bf16[4,1,64,128]{3,2,1,0:T(8,128)(2,1)S(1)} %stack.14), channel_id=1, replica_groups=mesh['dp_0'=4,'dp_1'=16,'mp'=8] {'dp_0'}, dimensions={0} | all-to-all | bytes 131072 | tf_op jit(solution)/shard_map/all_to_all | solution.py:21
  106.4 1.2 stack.15
  107.7 0.0 copy-start.3
  107.7 8.6 %all-to-all-start.5 = ((bf16[16,4,64,128]{3,2,1,0:T(8,128)(2,1)}), bf16[16,4,64,128]{3,2,1,0:T(8,128)(2,1)S(1)}, u32[]{:S(2)}, u32[]{:S(2)}) async-start(bf16[16,4,64,128]{3,2,1,0:T(8,128)(2,1)} %stack.15), calls=%async_computation.5 | async-start | bytes 2097152 | tf_op jit(solution)/shard_map/all_to_all | solution.py:21
  117.0 47.2 %all-to-all-done.5 = bf16[16,4,64,128]{3,2,1,0:T(8,128)(2,1)S(1)} async-done(((bf16[16,4,64,128]{3,2,1,0:T(8,128)(2,1)}), bf16[16,4,64,128]{3,2,1,0:T(8,128)(2,1)S(1)}, u32[]{:S(2)}, u32[]{:S(2)}) %all-to-all-start.5) | async-done | bytes 1048608 | tf_op jit(solution)/shard_map/all_to_all | solution.py:21
  164.2 0.0 copy-start.2
  164.2 0.1 copy.16
  164.3 0.0 copy-done.3
  164.3 1.5 copy-done.2
  165.8 1.1 fusion.9
  (8 shorter events, 0.1 us)
Async XLA Ops:
  0.0 75.5 %copy-start = (bf16[8192,128]{1,0:T(8,128)(2,1)S(1)}, bf16[8192,128]{1,0:T(8,128)(2,1)}, u32[]{:S(2)}) copy-start(bf16[8192,128]{1,0:T(8,128)(2,1)} %param.11) | copy-start | bytes 6291460
  0.0 26.8 %copy-start.5 = (s32[128,4]{0,1:T(4,128)S(1)}, s32[128,4]{0,1:T(4,128)}, u32[]{:S(2)}) copy-start(s32[128,4]{0,1:T(4,128)} %param.16) | copy-start | bytes 6148
  0.0 27.0 %copy-start.1 = (s32[128]{0:T(128)S(1)}, s32[128]{0:T(128)}, u32[]{:S(2)}) copy-start(s32[128]{0:T(128)} %param.17) | copy-start | bytes 1540
  12.0 62.5 %all-to-all-start.1 = ((bf16[16,4,64,128]{3,2,1,0:T(8,128)(2,1)}), bf16[16,4,64,128]{3,2,1,0:T(8,128)(2,1)S(1)}, u32[]{:S(2)}, u32[]{:S(2)}) async-start(bf16[16,4,64,128]{3,2,1,0:T(8,128)(2,1)} %stack.13), calls=%async_computation.1 | async-start | bytes 2097152 | tf_op jit(solution)/shard_map/all_to_all | solution.py:21
  74.9 0.8 copy-start.4
  75.6 11.6 %copy-start.6 = (bf16[16,64,128]{2,1,0:T(8,128)(2,1)S(1)}, bf16[16,64,128]{2,1,0:T(8,128)(2,1)}, u32[]{:S(2)}) copy-start(bf16[16,64,128]{2,1,0:T(8,128)(2,1)} %param.14) | copy-start | bytes 786436
  76.8 10.4 %all-to-all-start.2 = ((bf16[8,64,128]{2,1,0:T(8,128)(2,1)}), bf16[8,64,128]{2,1,0:T(8,128)(2,1)S(1)}, u32[]{:S(2)}, u32[]{:S(2)}) async-start(bf16[8,64,128]{2,1,0:T(8,128)(2,1)} %broadcast_in_dim.36), calls=%async_computation.2 | async-start | bytes 262144 | tf_op jit(solution)/shard_map/all_to_all | solution.py:35
  87.2 1.3 copy-start.7
  107.7 56.6 %copy-start.3 = (bf16[64,128]{1,0:T(8,128)(2,1)S(1)}, bf16[64,128]{1,0:T(8,128)(2,1)}, u32[]{:S(2)}) copy-start(bf16[64,128]{1,0:T(8,128)(2,1)} %param.9) | copy-start | bytes 49156
  107.7 56.5 %all-to-all-start.5 = ((bf16[16,4,64,128]{3,2,1,0:T(8,128)(2,1)}), bf16[16,4,64,128]{3,2,1,0:T(8,128)(2,1)S(1)}, u32[]{:S(2)}, u32[]{:S(2)}) async-start(bf16[16,4,64,128]{3,2,1,0:T(8,128)(2,1)} %stack.15), calls=%async_computation.5 | async-start | bytes 2097152 | tf_op jit(solution)/shard_map/all_to_all | solution.py:21
  164.2 1.6 copy-start.2
